TPU v7x, 32 devices: a whole 2x2x4 slice. The times are simulated.
32 devices in a mesh: grp: 4 (over y, x), chan: 8 (over z, core).
Axes of the slice: x: 2, y: 2, z: 4, core: 2. Of those that a mesh axis runs over, the one named last changes fastest.
Arguments:
- visibility: float32 [1024, 32768], P('chan', 'grp'), may hold values from -6 to 6
- interference_mask: int32 [1024, 16384], P(None, ('grp', 'chan')), may hold values from 0 to 1
- valid_time_count: int32 [512], P(('grp', 'chan')), may hold values from 8 to 32
- fit_modes: float32 [1024, 32], P('grp'), may hold values from -1 to 1
Outputs:
- residual_vis: float32 [1024, 32768], P('chan', 'grp')
All inputs are finite; a program needn't handle non-finite values.
Results may differ from a plain program's by a relative error of at most 0.0003.
Values sent between devices are 32-bit elements; how exact they have to be, the bound alone decides.
A program may use at most 128 MiB of HBM per device.

v0:
```python
import jax
import jax.numpy as jnp
from jax import lax
from jax.sharding import PartitionSpec as P

damping = 0.1


def fit_weight(interference_mask, valid_time_count):
    antenna_pairs_list = valid_time_count.shape[0]
    sample_values = interference_mask.shape[1] // antenna_pairs_list
    projection_sums = lax.broadcasted_iota(jnp.int32, (antenna_pairs_list, sample_values), 1)
    within_range = (
        (projection_sums < valid_time_count[:, None])
        .astype(jnp.float32)
        .reshape(1, antenna_pairs_list * sample_values)
    )
    return (1.0 - interference_mask.astype(jnp.float32)) * within_range


def solve_normal(normal_matrix, target_signal):
    span_length = normal_matrix.shape[0]
    trailing = normal_matrix
    columns = []
    for position in range(span_length):
        column = trailing[:, 0] / jnp.sqrt(trailing[0, 0])
        columns.append(column)
        trailing = trailing[1:, 1:] - column[1:, None, :] * column[None, 1:, :]
    remains = target_signal
    forward = []
    for position in range(span_length):
        column = columns[position]
        current = remains[0] / column[0][None, :]
        forward.append(current)
        remains = remains[1:] - column[1:, None, :] * current[None]
    solution_values = [None] * span_length
    for position in reversed(range(span_length)):
        column = columns[position]
        current = forward[position]
        if position + 1 < span_length:
            later_rows = jnp.stack(solution_values[position + 1 :], 0)
            current = current - jnp.sum(column[1:, None, :] * later_rows, axis=0)
        solution_values[position] = current / column[0][None, :]
    return jnp.stack(solution_values, 0)


def solve_amplitudes(spectral_templates, assigned_rows, sample_weight, antenna_pairs_list):
    channel_count, span_length = spectral_templates.shape
    sample_values = sample_weight.shape[1] // antenna_pairs_list
    pairs = (spectral_templates[:, :, None] * spectral_templates[:, None, :]).reshape(
        channel_count, span_length * span_length
    )
    normal_matrix = lax.dot_general(
        pairs,
        sample_weight,
        (((0,), (0,)), ((), ())),
        precision=lax.Precision.HIGHEST,
        preferred_element_type=jnp.float32,
    )
    normal_matrix = normal_matrix.reshape(
        span_length, span_length, antenna_pairs_list * sample_values
    )
    normal_matrix = (
        normal_matrix + damping * jnp.eye(span_length, dtype=normal_matrix.dtype)[:, :, None]
    )
    weighted_values = assigned_rows.reshape(
        channel_count, antenna_pairs_list, 2, sample_values
    ) * sample_weight.reshape(channel_count, antenna_pairs_list, 1, sample_values)
    weighted_values = weighted_values.reshape(channel_count, antenna_pairs_list * 2 * sample_values)
    template_projection = lax.dot_general(
        spectral_templates,
        weighted_values,
        (((0,), (0,)), ((), ())),
        precision=lax.Precision.HIGHEST,
        preferred_element_type=jnp.float32,
    )
    target_signal = (
        template_projection.reshape(span_length, antenna_pairs_list, 2, sample_values)
        .transpose(0, 2, 1, 3)
        .reshape(span_length, 2, antenna_pairs_list * sample_values)
    )
    solution_values = solve_normal(normal_matrix, target_signal)
    return (
        solution_values.reshape(span_length, 2, antenna_pairs_list, sample_values)
        .transpose(0, 2, 1, 3)
        .reshape(span_length, antenna_pairs_list * 2 * sample_values)
    )


def per_device(visibility, interference_mask, valid_time_count, fit_modes):
    spectral_templates = lax.all_gather(fit_modes, "grp", axis=0, tiled=True)
    assigned_rows = lax.all_to_all(visibility, "chan", split_axis=1, concat_axis=0, tiled=True)
    antenna_pairs_list = valid_time_count.shape[0]
    sample_weight = fit_weight(interference_mask, valid_time_count)
    mode_amplitudes = solve_amplitudes(
        spectral_templates, assigned_rows, sample_weight, antenna_pairs_list
    )
    local_rows = visibility.shape[0]
    local_basis = lax.dynamic_slice_in_dim(
        spectral_templates, lax.axis_index("chan") * local_rows, local_rows, 0
    )
    model = jnp.dot(
        local_basis,
        lax.all_gather(mode_amplitudes, "chan", axis=1, tiled=True),
        precision=lax.Precision.HIGHEST,
        preferred_element_type=jnp.float32,
    )
    return visibility - model


def solution(mesh):
    placed = (P("chan", "grp"), P(None, ("grp", "chan")), P(("grp", "chan")), P("grp", None))
    return jax.shard_map(
        per_device, mesh=mesh, in_specs=placed, out_specs=P("chan", "grp"), check_vma=False
    )
```

profile of v0, /device:TPU:0, one launch (start us, length us, event | category | flops | bytes accessed | tf_op | source)
XLA Modules:
  0.0 204.1 jit_solution(10742631934232733337)
XLA Ops:
  6.5 5.6 %copy.41 = f32[128,8192]{0,1:T(8,128)} copy(f32[128,8192]{1,0:T(8,128)} %param.4) | data formatting | bytes 8388608 | tf_op args[0]
  12.1 6.5 %all-to-all-start = ((f32[128,8,1024]{0,2,1:T(8,128)}), f32[128,8,1024]{0,2,1:T(8,128)}, u32[]{:S(2)}, u32[]{:S(2)}) async-start(f32[128,8,1024]{0,2,1:T(8,128)} %bitcast.362), calls=%async_computation | async-start | bytes 8388608 | tf_op jit(solution)/shard_map/all_to_all | solution.py:92
  18.8 8.5 %all_gather.6 = f32[1024,32]{0,1:T(8,128)S(1)} all-gather(f32[256,32]{0,1:T(8,128)S(1)} %copy-done.17), channel_id=1, replica_groups=mesh['grp'=4,'chan'=8] {'grp'}, dimensions={0}, use_global_device_ids=true | all-gather | bytes 163840 | tf_op jit(solution)/shard_map/all_gather | solution.py:91
  27.3 1.8 copy.43
  29.1 1.8 subtract_multiply_fusion
  30.9 6.7 %fusion.6 = f32[32,32,512]{2,1,0:T(8,128)S(1)} fusion(f32[1024,512]{0,1:T(8,128)S(1)} %subtract_multiply_fusion, f32[1024,32]{0,1:T(8,128)S(1)} %all_gather.6, f32[32,32]{1,0:T(8,128)S(1)} %fusion.13), kind=kOutput, calls=%fused_computation.16 | convolution fusion | flops 6444023808 | bytes 4329472 | tf_op jit(solution)/shard_map/dot_general | solution.py:53
  52.8 0.7 div.867
  53.5 2.5 %mul.536 = f32[1024,16,2,32]{0,3,2,1:T(8,128)} broadcast(f32[1024,16,32]{0,2,1:T(8,128)S(1)} %bitcast.364), dimensions={0,1,3} | broadcast | bytes 6291456 | tf_op jit(solution)/shard_map/mul | solution.py:66
  56.0 5.3 %copy.44 = f32[1024,1024]{1,0:T(8,128)} copy(f32[1024,1024]{0,1:T(8,128)} %bitcast.363) | data formatting | bytes 8388608 | tf_op jit(solution)/shard_map/mul | solution.py:66
  61.4 51.3 %all-to-all-done = f32[128,8,1024]{0,2,1:T(8,128)} async-done(((f32[128,8,1024]{0,2,1:T(8,128)}), f32[128,8,1024]{0,2,1:T(8,128)}, u32[]{:S(2)}, u32[]{:S(2)}) %all-to-all-start) | async-done | bytes 4194336 | tf_op jit(solution)/shard_map/all_to_all | solution.py:92
  112.7 5.3 %copy.42 = f32[8,128,1024]{2,1,0:T(8,128)} copy(f32[8,128,1024]{1,2,0:T(8,128)} %bitcast.1) | data formatting | bytes 8388608 | tf_op jit(solution)/shard_map/all_to_all | solution.py:92
  118.0 4.4 %bitcast_multiply_fusion = f32[1024,1024]{1,0:T(8,128)S(1)} fusion(f32[1024,1024]{1,0:T(8,128)} %copy.44, f32[8,128,1024]{2,1,0:T(8,128)} %copy.42), kind=kLoop, calls=%fused_computation.3 | loop fusion | flops 1048576 | bytes 12582912 | tf_op jit(solution)/shard_map/mul | solution.py:66
  122.4 2.6 %convolution_bitcast_fusion = f32[32,1024]{1,0:T(8,128)S(1)} fusion(f32[1024,1024]{1,0:T(8,128)S(1)} %bitcast_multiply_fusion, f32[1024,32]{0,1:T(8,128)S(1)} %all_gather.6), kind=kOutput, calls=%fused_computation.18 | convolution fusion | flops 402653184 | bytes 4456448 | tf_op jit(solution)/shard_map/dot_general | solution.py:70
  128.3 0.7 slice_subtract_fusion.58
  129.2 0.7 stack.184
  129.9 0.7 stack.183
  130.6 0.7 fusion.46
  131.4 0.7 stack.182
  132.0 0.7 fusion.45
  132.8 0.7 constant_dynamic-update-slice_fusion.4
  133.6 1.3 constant_dynamic-update-slice_fusion.10
  136.1 0.6 constant_dynamic-update-slice_fusion.7
  137.9 0.8 multiply_reduce_fusion.25
  138.7 1.3 constant_dynamic-update-slice_fusion.17
  140.0 0.7 stack.179
  141.8 0.6 constant_dynamic-update-slice_fusion.14
  144.2 0.8 multiply_reduce_fusion.24
  145.0 0.7 constant_dynamic-update-slice_fusion.25
  145.7 0.7 stack.178
  146.4 0.7 constant_dynamic-update-slice_fusion.34
  147.1 0.7 stack.177
  147.9 0.7 constant_dynamic-update-slice_fusion.44
  148.8 0.7 constant_dynamic-update-slice_fusion.55
  149.7 0.7 constant_dynamic-update-slice_fusion.67
  150.7 0.7 constant_dynamic-update-slice_fusion.80
  151.6 0.7 constant_dynamic-update-slice_fusion.94
  152.6 0.7 constant_dynamic-update-slice_fusion.109
  153.8 0.7 constant_dynamic-update-slice_fusion.142
  154.9 0.7 constant_dynamic-update-slice_fusion.160
  155.9 0.7 constant_dynamic-update-slice_fusion.179
  156.9 0.6 constant_dynamic-update-slice_fusion.199
  157.9 0.6 constant_dynamic-update-slice_fusion.220
  158.9 0.7 constant_dynamic-update-slice_fusion.242
  160.0 0.6 constant_dynamic-update-slice_fusion.265
  161.0 0.6 constant_dynamic-update-slice_fusion.289
  166.6 1.3 reshape.1023
  167.9 21.3 %all-gather.2.cloned.1.call-done = f32[32,8192]{1,0:T(8,128)} async-done(((f32[32,1024]{1,0:T(8,128)}), f32[32,8192]{1,0:T(8,128)}) %all-gather.2.cloned.1.call-update) | async-done | bytes 1048592 | tf_op jit(solution)/shard_map/all_gather | solution.py:104
  189.3 8.0 %convolution_subtract_fusion = f32[128,8192]{1,0:T(8,128)} fusion(f32[128,8192]{1,0:T(8,128)} %param.4, f32[32,8192]{1,0:T(8,128)} %all-gather.2.cloned.1.call-done, f32[1024,32]{0,1:T(8,128)S(1)} %all_gather.6, s32[]{:T(128)S(6)} %select_n.3), kind=kOutput, calls=%fused_computation | convolution fusion | flops 403701760 | bytes 9453572 | tf_op jit(solution)/shard_map/dot_general | solution.py:102
  (922 shorter events, 30.0 us)
Async XLA Ops:
  12.1 6.6 %copy-start.56 = (s32[16]{0:T(128)S(1)}, s32[16]{0:T(128)}, u32[]{:S(2)}) copy-start(s32[16]{0:T(128)} %param.6) | copy-start | bytes 196
  12.1 6.7 %copy-start.17 = (f32[256,32]{0,1:T(8,128)S(1)}, f32[256,32]{0,1:T(8,128)}, u32[]{:S(2)}) copy-start(f32[256,32]{0,1:T(8,128)} %param.7) | copy-start | bytes 98308
  12.1 15.2 %copy-start = (s32[1024,512]{1,0:T(8,128)S(1)}, s32[1024,512]{1,0:T(8,128)}, u32[]{:S(2)}) copy-start(s32[1024,512]{1,0:T(8,128)} %param.5) | copy-start | bytes 6291460
  12.1 100.6 %all-to-all-start = ((f32[128,8,1024]{0,2,1:T(8,128)}), f32[128,8,1024]{0,2,1:T(8,128)}, u32[]{:S(2)}, u32[]{:S(2)}) async-start(f32[128,8,1024]{0,2,1:T(8,128)} %bitcast.362), calls=%async_computation | async-start | bytes 8388608 | tf_op jit(solution)/shard_map/all_to_all | solution.py:92
  18.6 170.7 %all-gather.2.cloned.1.call-start = ((), (), s32[]{:S(2)}) async-start(), calls=%async_computation.1 | async-start | bytes 1179648 | tf_op jit(solution)/shard_map/all_gather | solution.py:104
  44.0 82.0 %copy-start.19 = (f32[1,512]{1,0:T(1,128)}, f32[1,512]{1,0:T(1,128)S(1)}, u32[]{:S(2)}) copy-start(f32[1,512]{1,0:T(1,128)S(1)} %slice.1010) | copy-start | bytes 6148
  44.0 82.1 %copy-start.21 = (f32[1,512]{1,0:T(1,128)}, f32[1,512]{1,0:T(1,128)S(1)}, u32[]{:S(2)}) copy-start(f32[1,512]{1,0:T(1,128)S(1)} %slice.1017) | copy-start | bytes 6148
  44.0 82.2 %copy-start.23 = (f32[1,512]{1,0:T(1,128)}, f32[1,512]{1,0:T(1,128)S(1)}, u32[]{:S(2)}) copy-start(f32[1,512]{1,0:T(1,128)S(1)} %slice.1024) | copy-start | bytes 6148
  44.0 82.3 %copy-start.25 = (f32[1,512]{1,0:T(1,128)}, f32[1,512]{1,0:T(1,128)S(1)}, u32[]{:S(2)}) copy-start(f32[1,512]{1,0:T(1,128)S(1)} %slice.1031) | copy-start | bytes 6148
  44.1 82.4 %copy-start.27 = (f32[1,512]{1,0:T(1,128)}, f32[1,512]{1,0:T(1,128)S(1)}, u32[]{:S(2)}) copy-start(f32[1,512]{1,0:T(1,128)S(1)} %slice.1038) | copy-start | bytes 6148
  44.1 82.5 %copy-start.29 = (f32[1,512]{1,0:T(1,128)}, f32[1,512]{1,0:T(1,128)S(1)}, u32[]{:S(2)}) copy-start(f32[1,512]{1,0:T(1,128)S(1)} %slice.1045) | copy-start | bytes 6148
  44.1 82.6 %copy-start.31 = (f32[1,512]{1,0:T(1,128)}, f32[1,512]{1,0:T(1,128)S(1)}, u32[]{:S(2)}) copy-start(f32[1,512]{1,0:T(1,128)S(1)} %slice.1052) | copy-start | bytes 6148
  44.1 82.7 %copy-start.33 = (f32[1,512]{1,0:T(1,128)}, f32[1,512]{1,0:T(1,128)S(1)}, u32[]{:S(2)}) copy-start(f32[1,512]{1,0:T(1,128)S(1)} %slice.1059) | copy-start | bytes 6148
  44.1 82.8 %copy-start.34 = (f32[1,512]{1,0:T(1,128)}, f32[1,512]{1,0:T(1,128)S(1)}, u32[]{:S(2)}) copy-start(f32[1,512]{1,0:T(1,128)S(1)} %slice.1066) | copy-start | bytes 6148
  44.2 82.8 %copy-start.35 = (f32[1,512]{1,0:T(1,128)}, f32[1,512]{1,0:T(1,128)S(1)}, u32[]{:S(2)}) copy-start(f32[1,512]{1,0:T(1,128)S(1)} %slice.1073) | copy-start | bytes 6148
  44.2 82.9 %copy-start.36 = (f32[1,512]{1,0:T(1,128)}, f32[1,512]{1,0:T(1,128)S(1)}, u32[]{:S(2)}) copy-start(f32[1,512]{1,0:T(1,128)S(1)} %slice.1080) | copy-start | bytes 6148
  44.2 82.9 %copy-start.37 = (f32[1,512]{1,0:T(1,128)}, f32[1,512]{1,0:T(1,128)S(1)}, u32[]{:S(2)}) copy-start(f32[1,512]{1,0:T(1,128)S(1)} %slice.1087) | copy-start | bytes 6148
  44.2 83.0 %copy-start.38 = (f32[1,512]{1,0:T(1,128)}, f32[1,512]{1,0:T(1,128)S(1)}, u32[]{:S(2)}) copy-start(f32[1,512]{1,0:T(1,128)S(1)} %slice.1094) | copy-start | bytes 6148
  44.2 83.0 %copy-start.39 = (f32[1,512]{1,0:T(1,128)}, f32[1,512]{1,0:T(1,128)S(1)}, u32[]{:S(2)}) copy-start(f32[1,512]{1,0:T(1,128)S(1)} %slice.1101) | copy-start | bytes 6148
  44.3 83.1 %copy-start.40 = (f32[1,512]{1,0:T(1,128)}, f32[1,512]{1,0:T(1,128)S(1)}, u32[]{:S(2)}) copy-start(f32[1,512]{1,0:T(1,128)S(1)} %slice.1108) | copy-start | bytes 6148
  44.3 83.2 %copy-start.41 = (f32[1,512]{1,0:T(1,128)}, f32[1,512]{1,0:T(1,128)S(1)}, u32[]{:S(2)}) copy-start(f32[1,512]{1,0:T(1,128)S(1)} %slice.1115) | copy-start | bytes 6148
  52.1 3.9 %copy-start.9 = (f32[3,3,512]{2,1,0:T(4,128)}, f32[3,3,512]{2,1,0:T(4,128)S(1)}, u32[]{:S(2)}) copy-start(f32[3,3,512]{2,1,0:T(4,128)S(1)} %slice_subtract_fusion.52) | copy-start | bytes 55300
  126.3 1.5 copy-start.46
  126.4 1.5 copy-start.48
  126.5 1.5 copy-start.49
  126.5 1.5 copy-start.50
  126.5 1.6 copy-start.51
  126.5 1.6 copy-start.52
  126.6 1.6 copy-start.53
  126.6 1.6 copy-start.54
  126.6 1.6 copy-start.55
  127.6 1.6 copy-start.1
  127.7 1.5 copy-start.2
  134.9 18.7 %copy-start.42 = (f32[1,512]{1,0:T(1,128)S(1)}, f32[1,512]{1,0:T(1,128)}, u32[]{:S(2)}) copy-start(f32[1,512]{1,0:T(1,128)} %copy-done.41) | copy-start | bytes 6148
  150.6 11.4 %copy-start.32 = (f32[1,512]{1,0:T(1,128)S(1)}, f32[1,512]{1,0:T(1,128)}, u32[]{:S(2)}) copy-start(f32[1,512]{1,0:T(1,128)} %copy-done.31) | copy-start | bytes 6148
  152.4 10.1 %copy-start.30 = (f32[1,512]{1,0:T(1,128)S(1)}, f32[1,512]{1,0:T(1,128)}, u32[]{:S(2)}) copy-start(f32[1,512]{1,0:T(1,128)} %copy-done.29) | copy-start | bytes 6148
  153.6 9.4 %copy-start.28 = (f32[1,512]{1,0:T(1,128)S(1)}, f32[1,512]{1,0:T(1,128)}, u32[]{:S(2)}) copy-start(f32[1,512]{1,0:T(1,128)} %copy-done.27) | copy-start | bytes 6148
  154.8 8.7 %copy-start.26 = (f32[1,512]{1,0:T(1,128)S(1)}, f32[1,512]{1,0:T(1,128)}, u32[]{:S(2)}) copy-start(f32[1,512]{1,0:T(1,128)} %copy-done.25) | copy-start | bytes 6148
  156.6 7.3 %copy-start.24 = (f32[1,512]{1,0:T(1,128)S(1)}, f32[1,512]{1,0:T(1,128)}, u32[]{:S(2)}) copy-start(f32[1,512]{1,0:T(1,128)} %copy-done.23) | copy-start | bytes 6148
  157.8 6.7 %copy-start.22 = (f32[1,512]{1,0:T(1,128)S(1)}, f32[1,512]{1,0:T(1,128)}, u32[]{:S(2)}) copy-start(f32[1,512]{1,0:T(1,128)} %copy-done.21) | copy-start | bytes 6148
  158.9 6.1 %copy-start.20 = (f32[1,512]{1,0:T(1,128)S(1)}, f32[1,512]{1,0:T(1,128)}, u32[]{:S(2)}) copy-start(f32[1,512]{1,0:T(1,128)} %copy-done.19) | copy-start | bytes 6148
  160.8 4.9 %copy-start.18 = (f32[16,32]{1,0:T(8,128)S(1)}, f32[16,32]{1,0:T(8,128)}, u32[]{:S(2)}) copy-start(f32[16,32]{1,0:T(8,128)} %div.867) | copy-start | bytes 6148
  162.3 3.6 %copy-start.16 = (f32[1,2,16,32]{3,2,1,0:T(8,128)S(1)}, f32[1,2,16,32]{3,2,1,0:T(8,128)}, u32[]{:S(2)}) copy-start(f32[1,2,16,32]{3,2,1,0:T(8,128)} %stack.177) | copy-start | bytes 12292
  162.4 3.6 %copy-start.15 = (f32[1,2,16,32]{3,2,1,0:T(8,128)S(1)}, f32[1,2,16,32]{3,2,1,0:T(8,128)}, u32[]{:S(2)}) copy-start(f32[1,2,16,32]{3,2,1,0:T(8,128)} %stack.178) | copy-start | bytes 12292
  162.4 3.6 %copy-start.14 = (f32[1,2,16,32]{3,2,1,0:T(8,128)S(1)}, f32[1,2,16,32]{3,2,1,0:T(8,128)}, u32[]{:S(2)}) copy-start(f32[1,2,16,32]{3,2,1,0:T(8,128)} %stack.179) | copy-start | bytes 12292
  162.5 3.7 %copy-start.13 = (f32[1,2,16,32]{3,2,1,0:T(8,128)S(1)}, f32[1,2,16,32]{3,2,1,0:T(8,128)}, u32[]{:S(2)}) copy-start(f32[1,2,16,32]{3,2,1,0:T(8,128)} %stack.182) | copy-start | bytes 12292
  162.5 3.8 %copy-start.12 = (f32[1,2,16,32]{3,2,1,0:T(8,128)S(1)}, f32[1,2,16,32]{3,2,1,0:T(8,128)}, u32[]{:S(2)}) copy-start(f32[1,2,16,32]{3,2,1,0:T(8,128)} %stack.183) | copy-start | bytes 12292
  162.5 3.7 %copy-start.11 = (f32[1,2,16,32]{3,2,1,0:T(8,128)S(1)}, f32[1,2,16,32]{3,2,1,0:T(8,128)}, u32[]{:S(2)}) copy-start(f32[1,2,16,32]{3,2,1,0:T(8,128)} %stack.184) | copy-start | bytes 12292
  (11 other events, 14.4 us)
Sparse Core Ops, SparseCore 0:
  168.1 21.1 all-gather.1
where the time goes:
time: 205 us; the launch traced here: 204 us
  waiting for transfers between devices  72.7 us (35%)
  local copies, waits for them, and re-layouts  49.4 us (24%)
  other arithmetic  32.3 us (16%)
  between operations  17.4 us (8%)
  matrix products  17.3 us (8%)
  blocking collectives  8.45 us (4%)
  starting transfers between devices  6.53 us (3%)
    all_to_all x1, waiting for transfers between devices, per_device(): lax.all_to_all(visibility, 'chan', split_axis=1, concat_axis=0, tiled=True)  51.3 us
    all_gather x1, waiting for transfers between devices, per_device(): lax.all_gather(mode_amplitudes, 'chan', axis=1, tiled=True)  21.3 us
    unnamed x578, local copies, waits for them, and re-layouts  16.9 us
    unnamed x28, other arithmetic  14.1 us
    all_gather x1, blocking collectives, per_device(): spectral_templates = lax.all_gather(fit_modes, 'grp', axis=0, tiled=True)  8.45 us
    dot_general x1, matrix products, per_device(): jnp.dot(local_basis, lax.all_gather(mode_amplitudes, 'chan', axis=1, tile...  8 us
    mul x2, local copies, waits for them, and re-layouts, solve_amplitudes(): assigned_rows.reshape(channel_count, antenna_pairs_list, 2, sample_values)  7.88 us
    slice x32, local copies, waits for them, and re-layouts, solve_normal(): current = remains[0] / column[0][None, :]  7.51 us
  transfers between devices with their start and end apart: 2, of which 2 were waited for; matrix products, arithmetic and copies ran while one was open for 16% of the time, Pallas kernels for 0%

commit v1 on v0

--- a/solution.py
+++ b/solution.py
@@ -1,9 +1,22 @@
+import functools
 import jax
 import jax.numpy as jnp
 from jax import lax
 from jax.sharding import PartitionSpec as P
 
 damping = 0.1
+
+
+def _play_figure(q_in, mesh_ax):
+    ready = lax.axis_size(mesh_ax)
+    last = jnp.split(q_in, ready, axis=1)
+    right_arr = jnp.stack(last)
+    return jnp.concatenate(
+        lax.all_to_all(right_arr, axis_name=mesh_ax, split_axis=0, concat_axis=0), axis=0
+    )
+
+
+compute_face = functools.partial(_play_figure, mesh_ax="chan")
 
 
 def fit_weight(interference_mask, valid_time_count):
@@ -89,7 +102,7 @@
 
 def per_device(visibility, interference_mask, valid_time_count, fit_modes):
     spectral_templates = lax.all_gather(fit_modes, "grp", axis=0, tiled=True)
-    assigned_rows = lax.all_to_all(visibility, "chan", split_axis=1, concat_axis=0, tiled=True)
+    assigned_rows = compute_face(visibility)
     antenna_pairs_list = valid_time_count.shape[0]
     sample_weight = fit_weight(interference_mask, valid_time_count)
     mode_amplitudes = solve_amplitudes(

time: 205 us -> 249 us (1.21)
  local copies, waits for them, and re-layouts: 49.4 us -> 87.9 us
  other arithmetic: 32.3 us -> 38.9 us
  waiting for transfers between devices: 72.7 us -> 69.5 us
    unnamed x578 -> x622, local copies, waits for them, and re-layouts: 16.9 us -> 49.5 us
    slice x32, local copies, waits for them, and re-layouts: 7.51 us -> 17.5 us  [solve_normal(): current = remains[0] / column[0][None, :]]
    mul x2 -> x0, local copies, waits for them, and re-layouts: 7.88 us -> none  [solve_amplitudes(): assigned_rows.reshape(channel_count, antenna_pairs_list, 2, sample_values)]
    another operation x0 -> x2, local copies, waits for them, and re-layouts: none -> 7.22 us  [the longest x1 5.34 us: solve_amplitudes(): assigned_rows.reshape(channel_count, antenna_pairs_list, 2, sample_values)]
    all_to_all x1 -> x0, local copies, waits for them, and re-layouts: 5.34 us -> none  [per_device(): lax.all_to_all(visibility, 'chan', split_axis=1, concat_axis=0, tiled=True)]
    unnamed x28, other arithmetic: 14.1 us -> 18.6 us
    reduce_sum x30, other arithmetic: 3.05 us -> 6.94 us  [solve_normal(): current = current - jnp.sum(column[1:, None, :] * later_rows, axis=0)]
    all_to_all x1, waiting for transfers between devices: 51.3 us -> 48.2 us  [_play_figure(): lax.all_to_all(right_arr, axis_name=mesh_ax, split_axis=0, concat_axis=0)]
  transfers between devices with their start and end apart: 2 -> 2, of which waited for: 2 -> 2; matrix products, arithmetic and copies ran while one was open for 16% -> 14% of each run, Pallas kernels for 0% -> 0%
where the time goes in v1:
time: 249 us; the launch traced here: 247 us
  local copies, waits for them, and re-layouts  87.9 us (35%)
  waiting for transfers between devices  69.5 us (28%)
  other arithmetic  38.9 us (16%)
  matrix products  18.7 us (8%)
  between operations  17.5 us (7%)
  blocking collectives  8.45 us (3%)
  starting transfers between devices  6.52 us (3%)
    unnamed x622, local copies, waits for them, and re-layouts  49.5 us
    all_to_all x1, waiting for transfers between devices, _play_figure(): lax.all_to_all(right_arr, axis_name=mesh_ax, split_axis=0, concat_axis=0)  48.2 us
    all_gather x1, waiting for transfers between devices, per_device(): lax.all_gather(mode_amplitudes, 'chan', axis=1, tiled=True)  21.3 us
    unnamed x28, other arithmetic  18.6 us
    slice x32, local copies, waits for them, and re-layouts, solve_normal(): current = remains[0] / column[0][None, :]  17.5 us
    all_gather x1, blocking collectives, per_device(): spectral_templates = lax.all_gather(fit_modes, 'grp', axis=0, tiled=True)  8.45 us
    dot_general x1, matrix products, per_device(): jnp.dot(local_basis, lax.all_gather(mode_amplitudes, 'chan', axis=1, tile...  8.01 us
    reduce_sum x30, other arithmetic, solve_normal(): current = current - jnp.sum(column[1:, None, :] * later_rows, axis=0)  6.94 us
  transfers between devices with their start and end apart: 2, of which 2 were waited for; matrix products, arithmetic and copies ran while one was open for 14% of the time, Pallas kernels for 0%

profile of v1, /device:TPU:0, one launch (start us, length us, event | category | flops | bytes accessed | tf_op | source)
XLA Modules:
  0.0 247.4 jit_solution(5202021273358835567)
XLA Ops:
  6.5 1.9 constant_dynamic-update-slice_fusion.7
  8.4 1.9 constant_dynamic-update-slice_fusion.6
  10.3 1.9 constant_dynamic-update-slice_fusion.5
  12.2 1.9 constant_dynamic-update-slice_fusion.4
  14.1 1.9 constant_dynamic-update-slice_fusion.3
  16.0 1.9 constant_dynamic-update-slice_fusion.2
  17.8 1.9 constant_dynamic-update-slice_fusion.1
  19.7 1.9 constant_dynamic-update-slice_fusion
  21.6 6.5 %all-to-all-start = ((f32[8,128,1024]{2,1,0:T(8,128)}), f32[8,128,1024]{2,1,0:T(8,128)}, u32[]{:S(2)}, u32[]{:S(2)}) async-start(f32[8,128,1024]{2,1,0:T(8,128)} %constant_dynamic-update-slice_fusion), calls=%async_computation | async-start | bytes 8388608 | tf_op jit(solution)/shard_map/all_to_all | solution.py:15
  28.3 8.5 %all_gather.6 = f32[1024,32]{0,1:T(8,128)S(1)} all-gather(f32[256,32]{0,1:T(8,128)S(1)} %copy-done.38), channel_id=1, replica_groups=mesh['grp'=4,'chan'=8] {'grp'}, dimensions={0}, use_global_device_ids=true | all-gather | bytes 163840 | tf_op jit(solution)/shard_map/all_gather | solution.py:104
  36.8 1.9 copy.42
  38.7 1.8 subtract_multiply_fusion
  40.5 6.7 %fusion.6 = f32[32,32,512]{2,1,0:T(8,128)S(1)} fusion(f32[1024,512]{0,1:T(8,128)S(1)} %subtract_multiply_fusion, f32[1024,32]{0,1:T(8,128)S(1)} %all_gather.6, f32[32,32]{1,0:T(8,128)S(1)} %fusion.13), kind=kOutput, calls=%fused_computation.16 | convolution fusion | flops 6444023808 | bytes 4329472 | tf_op jit(solution)/shard_map/dot_general | solution.py:66
  74.0 48.2 %all-to-all-done = f32[8,128,1024]{2,1,0:T(8,128)} async-done(((f32[8,128,1024]{2,1,0:T(8,128)}), f32[8,128,1024]{2,1,0:T(8,128)}, u32[]{:S(2)}, u32[]{:S(2)}) %all-to-all-start) | async-done | bytes 4194336 | tf_op jit(solution)/shard_map/all_to_all | solution.py:15
  122.2 5.3 %copy.47 = f32[1024,1024]{0,1:T(8,128)} copy(f32[1024,1024]{1,0:T(8,128)} %bitcast.8) | data formatting | bytes 8388608 | tf_op jit(solution)/shard_map/reshape;reshape | solution.py:79
  127.6 2.7 %bitcast_multiply_fusion = f32[1024,1024]{0,1:T(8,128)S(1)} fusion(f32[1024,1024]{0,1:T(8,128)} %copy.47, f32[1024,16,32]{0,2,1:T(8,128)S(1)} %bitcast.376), kind=kLoop, calls=%fused_computation.3 | loop fusion | flops 1048576 | bytes 10485760 | tf_op jit(solution)/shard_map/mul | solution.py:79
  130.3 3.9 %convolution_bitcast_fusion = f32[32,1024]{1,0:T(8,128)S(1)} fusion(f32[1024,1024]{0,1:T(8,128)S(1)} %bitcast_multiply_fusion, f32[1024,32]{0,1:T(8,128)S(1)} %copy-done.18), kind=kOutput, calls=%fused_computation.18 | convolution fusion | flops 402653184 | bytes 4456448 | tf_op jit(solution)/shard_map/dot_general | solution.py:83
  137.9 0.7 slice_subtract_fusion.58
  138.8 0.7 stack.211
  140.2 0.7 fusion.46
  140.9 0.7 stack.209
  141.6 0.7 fusion.45
  143.0 0.7 constant_dynamic-update-slice_fusion.12
  143.7 1.3 constant_dynamic-update-slice_fusion.18
  148.1 0.8 multiply_reduce_fusion.25
  148.9 1.3 constant_dynamic-update-slice_fusion.25
  150.1 0.7 stack.206
  154.4 0.8 multiply_reduce_fusion.24
  155.1 1.3 constant_dynamic-update-slice_fusion.33
  160.6 0.8 multiply_reduce_fusion.23
  161.4 1.3 constant_dynamic-update-slice_fusion.42
  167.5 0.8 multiply_reduce_fusion.22
  168.3 1.3 constant_dynamic-update-slice_fusion.52
  175.0 0.8 multiply_reduce_fusion.21
  175.8 1.3 constant_dynamic-update-slice_fusion.63
  183.1 0.8 multiply_reduce_fusion.20
  183.9 1.3 constant_dynamic-update-slice_fusion.75
  191.8 0.8 multiply_reduce_fusion.19
  192.6 0.7 constant_dynamic-update-slice_fusion.88
  196.4 0.7 constant_dynamic-update-slice_fusion.150
  197.4 0.7 constant_dynamic-update-slice_fusion.168
  198.4 0.7 constant_dynamic-update-slice_fusion.187
  199.5 0.7 constant_dynamic-update-slice_fusion.207
  200.5 0.7 constant_dynamic-update-slice_fusion.228
  204.7 0.7 constant_dynamic-update-slice_fusion.322
  209.9 1.3 reshape.1015
  211.3 21.3 %all-gather.2.cloned.1.call-done = f32[32,8192]{1,0:T(8,128)} async-done(((f32[32,1024]{1,0:T(8,128)}), f32[32,8192]{1,0:T(8,128)}) %all-gather.2.cloned.1.call-update) | async-done | bytes 1048592 | tf_op jit(solution)/shard_map/all_gather | solution.py:117
  232.6 8.0 %convolution_subtract_fusion = f32[128,8192]{1,0:T(8,128)} fusion(f32[128,8192]{1,0:T(8,128)} %param.4, f32[32,8192]{1,0:T(8,128)} %all-gather.2.cloned.1.call-done, f32[1024,32]{0,1:T(8,128)} %copy-done.17, s32[]{:T(128)S(6)} %select_n.3), kind=kOutput, calls=%fused_computation | convolution fusion | flops 403701760 | bytes 9453572 | tf_op jit(solution)/shard_map/dot_general | solution.py:115
  (965 shorter events, 74.5 us)
Async XLA Ops:
  21.6 6.6 %copy-start.75 = (s32[16]{0:T(128)S(1)}, s32[16]{0:T(128)}, u32[]{:S(2)}) copy-start(s32[16]{0:T(128)} %param.6) | copy-start | bytes 196
  21.6 6.7 %copy-start.38 = (f32[256,32]{0,1:T(8,128)S(1)}, f32[256,32]{0,1:T(8,128)}, u32[]{:S(2)}) copy-start(f32[256,32]{0,1:T(8,128)} %param.7) | copy-start | bytes 98308
  21.6 15.2 %copy-start = (s32[1024,512]{1,0:T(8,128)S(1)}, s32[1024,512]{1,0:T(8,128)}, u32[]{:S(2)}) copy-start(s32[1024,512]{1,0:T(8,128)} %param.5) | copy-start | bytes 6291460
  21.6 100.6 %all-to-all-start = ((f32[8,128,1024]{2,1,0:T(8,128)}), f32[8,128,1024]{2,1,0:T(8,128)}, u32[]{:S(2)}, u32[]{:S(2)}) async-start(f32[8,128,1024]{2,1,0:T(8,128)} %constant_dynamic-update-slice_fusion), calls=%async_computation | async-start | bytes 8388608 | tf_op jit(solution)/shard_map/all_to_all | solution.py:15
  28.1 204.5 %all-gather.2.cloned.1.call-start = ((), (), s32[]{:S(2)}) async-start(), calls=%async_computation.1 | async-start | bytes 1179648 | tf_op jit(solution)/shard_map/all_gather | solution.py:117
  36.8 3.7 %copy-start.17 = (f32[1024,32]{0,1:T(8,128)}, f32[1024,32]{0,1:T(8,128)S(1)}, u32[]{:S(2)}) copy-start(f32[1024,32]{0,1:T(8,128)S(1)} %all_gather.6) | copy-start | bytes 393220
  54.7 13.4 %copy-start.1 = (f32[13,512]{1,0:T(8,128)}, f32[13,512]{1,0:T(8,128)S(1)}, u32[]{:S(2)}) copy-start(f32[13,512]{1,0:T(8,128)S(1)} %slice.1130) | copy-start | bytes 79876
  66.6 5.4 %copy-start.9 = (f32[11,512]{1,0:T(8,128)}, f32[11,512]{1,0:T(8,128)S(1)}, u32[]{:S(2)}) copy-start(f32[11,512]{1,0:T(8,128)S(1)} %slice.1144) | copy-start | bytes 67588
  67.4 60.2 %copy-start.13 = (f32[10,512]{1,0:T(8,128)}, f32[10,512]{1,0:T(8,128)S(1)}, u32[]{:S(2)}) copy-start(f32[10,512]{1,0:T(8,128)S(1)} %slice.1151) | copy-start | bytes 61444
  68.1 59.5 %copy-start.5 = (f32[9,512]{1,0:T(8,128)}, f32[9,512]{1,0:T(8,128)S(1)}, u32[]{:S(2)}) copy-start(f32[9,512]{1,0:T(8,128)S(1)} %slice.1158) | copy-start | bytes 55300
  70.6 67.0 %copy-start.19 = (f32[6,512]{1,0:T(8,128)}, f32[6,512]{1,0:T(8,128)S(1)}, u32[]{:S(2)}) copy-start(f32[6,512]{1,0:T(8,128)S(1)} %slice.1179) | copy-start | bytes 36868
  71.3 56.2 %copy-start.22 = (f32[5,512]{1,0:T(8,128)}, f32[5,512]{1,0:T(8,128)S(1)}, u32[]{:S(2)}) copy-start(f32[5,512]{1,0:T(8,128)S(1)} %slice.1186) | copy-start | bytes 30724
  72.7 54.8 %copy-start.31 = (f32[3,3,512]{2,1,0:T(4,128)}, f32[3,3,512]{2,1,0:T(4,128)S(1)}, u32[]{:S(2)}) copy-start(f32[3,3,512]{2,1,0:T(4,128)S(1)} %slice_subtract_fusion.52) | copy-start | bytes 55300
  127.5 2.8 %copy-start.18 = (f32[1024,32]{0,1:T(8,128)S(1)}, f32[1024,32]{0,1:T(8,128)}, u32[]{:S(2)}) copy-start(f32[1024,32]{0,1:T(8,128)} %copy-done.17) | copy-start | bytes 393220
  134.9 1.6 copy-start.55
  134.9 1.7 copy-start.56
  135.0 1.7 copy-start.57
  135.3 1.6 copy-start.60
  135.5 1.6 copy-start.62
  135.5 1.6 copy-start.63
  135.6 1.6 copy-start.12
  135.6 1.6 copy-start.64
  135.6 1.7 copy-start.10
  135.7 1.6 copy-start.65
  135.7 1.6 copy-start.14
  135.7 1.7 copy-start.66
  135.7 1.7 copy-start.6
  135.8 1.6 copy-start.67
  135.8 1.7 copy-start.68
  135.9 1.7 copy-start.21
  135.9 1.7 copy-start.69
  136.0 1.7 copy-start.70
  136.0 1.7 copy-start.23
  136.0 1.8 copy-start.71
  136.0 1.8 copy-start.72
  136.0 1.8 copy-start.73
  137.7 1.8 copy-start.29
  193.4 12.5 %copy-start.50 = (f32[1,512]{1,0:T(1,128)S(1)}, f32[1,512]{1,0:T(1,128)}, u32[]{:S(2)}) copy-start(f32[1,512]{1,0:T(1,128)} %slice.1045) | copy-start | bytes 6148
  195.2 11.2 %copy-start.48 = (f32[1,512]{1,0:T(1,128)S(1)}, f32[1,512]{1,0:T(1,128)}, u32[]{:S(2)}) copy-start(f32[1,512]{1,0:T(1,128)} %slice.1038) | copy-start | bytes 6148
  196.4 10.5 %copy-start.46 = (f32[1,512]{1,0:T(1,128)S(1)}, f32[1,512]{1,0:T(1,128)}, u32[]{:S(2)}) copy-start(f32[1,512]{1,0:T(1,128)} %slice.1031) | copy-start | bytes 6148
  198.2 9.1 %copy-start.44 = (f32[1,512]{1,0:T(1,128)S(1)}, f32[1,512]{1,0:T(1,128)}, u32[]{:S(2)}) copy-start(f32[1,512]{1,0:T(1,128)} %slice.1024) | copy-start | bytes 6148
  199.4 8.4 %copy-start.42 = (f32[1,512]{1,0:T(1,128)S(1)}, f32[1,512]{1,0:T(1,128)}, u32[]{:S(2)}) copy-start(f32[1,512]{1,0:T(1,128)} %slice.1017) | copy-start | bytes 6148
  201.3 7.1 %copy-start.40 = (f32[1,512]{1,0:T(1,128)S(1)}, f32[1,512]{1,0:T(1,128)}, u32[]{:S(2)}) copy-start(f32[1,512]{1,0:T(1,128)} %slice.1010) | copy-start | bytes 6148
  204.7 4.8 %copy-start.37 = (f32[1,2,16,32]{3,2,1,0:T(8,128)S(1)}, f32[1,2,16,32]{3,2,1,0:T(8,128)}, u32[]{:S(2)}) copy-start(f32[1,2,16,32]{3,2,1,0:T(8,128)} %stack.206) | copy-start | bytes 12292
  205.5 4.0 %copy-start.36 = (f32[1,2,16,32]{3,2,1,0:T(8,128)S(1)}, f32[1,2,16,32]{3,2,1,0:T(8,128)}, u32[]{:S(2)}) copy-start(f32[1,2,16,32]{3,2,1,0:T(8,128)} %stack.208) | copy-start | bytes 12292
  205.6 4.0 %copy-start.35 = (f32[1,2,16,32]{3,2,1,0:T(8,128)S(1)}, f32[1,2,16,32]{3,2,1,0:T(8,128)}, u32[]{:S(2)}) copy-start(f32[1,2,16,32]{3,2,1,0:T(8,128)} %stack.209) | copy-start | bytes 12292
  205.6 3.9 %copy-start.34 = (f32[1,2,16,32]{3,2,1,0:T(8,128)S(1)}, f32[1,2,16,32]{3,2,1,0:T(8,128)}, u32[]{:S(2)}) copy-start(f32[1,2,16,32]{3,2,1,0:T(8,128)} %stack.210) | copy-start | bytes 12292
  205.7 3.9 %copy-start.33 = (f32[1,2,16,32]{3,2,1,0:T(8,128)S(1)}, f32[1,2,16,32]{3,2,1,0:T(8,128)}, u32[]{:S(2)}) copy-start(f32[1,2,16,32]{3,2,1,0:T(8,128)} %stack.211) | copy-start | bytes 12292
  (30 other events, 37.3 us)
Sparse Core Ops, SparseCore 0:
  211.4 21.1 all-gather.1
